TPU v7x, 32 devices: a whole 2x2x4 slice. The times are simulated.
32 devices in a mesh: groups: 2 (over y), seq: 4 (over z), exp: 2 (over x), tp: 2 (over core).
Axes of the slice: x: 2, y: 2, z: 4, core: 2. Of those that a mesh axis runs over, the one named last changes fastest.
Arguments:
- attn_query: bfloat16 [2048, 1152], P(('groups', 'seq'), ('exp', 'tp')), parts along dimension 0, may hold values from -6 to 6
- fresh_keys: bfloat16 [2048, 1152], P(('groups', 'seq'), ('exp', 'tp')), parts along dimension 0, may hold values from -6 to 6
- fresh_values: bfloat16 [2048, 1152], P(('groups', 'seq'), ('exp', 'tp')), parts along dimension 0, may hold values from -6 to 6
- stale_keys: bfloat16 [2048, 1152], P(('groups', 'seq'), ('exp', 'tp')), parts along dimension 0, may hold values from -6 to 6
- stale_values: bfloat16 [2048, 1152], P(('groups', 'seq'), ('exp', 'tp')), parts along dimension 0, may hold values from -6 to 6
- block_flags: int32 [16], P(('groups', 'seq')), parts along dimension 0, may hold values 0 or 1
- moe_tokens: bfloat16 [4096, 1152], P(('groups', 'seq', 'exp', 'tp')), parts along dimension 0, may hold values from -6 to 6
- expert_ids: int32 [4096, 2], P(('groups', 'seq', 'exp', 'tp')), parts along dimension 0, may hold values from 0 to 3, all different within a row; in each aligned block of 128 rows (0 to 127, 128 to 255, ...) at most 80 rows name the same one
- gate_weights: float32 [4096, 2], P(('groups', 'seq', 'exp', 'tp')), parts along dimension 0, may hold values from 0.25 to 1
- up_weight: bfloat16 [4, 1152, 4608], P('seq', None, ('exp', 'tp')), may hold values from -0.1875 to 0.1875
- up_bias: float32 [4, 4608], P('seq', ('exp', 'tp')), may hold values from -3 to 3
- down_weight: bfloat16 [4, 4608, 1152], P('seq', ('exp', 'tp')), may hold values from -0.09375 to 0.09375
- down_bias: float32 [4, 1152], P('seq'), may hold values from -2 to 2
Outputs:
- attn_out: bfloat16 [2048, 1152], P(('groups', 'seq'), ('exp', 'tp')), parts along dimension 0
- moe_out: bfloat16 [4096, 1152], P(('groups', 'seq', 'exp', 'tp')), parts along dimension 0
There are 2 independent parts, one for each index of `groups`. A program takes and returns all parts, laid end to end along the dimension named above; an argument that names none is the same for every part. Nothing has to cross between parts.
Inputs may be any that keep to these rules, and one draw needn't show every extreme that they name: `expert_ids`: the 2 ids of a token differ. In the rows of one device no expert is named more than 80 times, and in every draw some expert is named exactly 80 times in some device's rows.
All inputs are finite; a program needn't handle non-finite values. No bound on the sum of `block_flags` on one device may be relied on, other than what follows from the above.
Results may differ from a plain program's by a relative error of at most 0.014.
Values may be sent and summed in bfloat16 or wider, within the bound.
A program may use at most 64 MiB of HBM per device.

v0:
```python
import math
import jax
import jax.numpy as jnp
from jax import lax
from jax.sharding import PartitionSpec as P

HD = 72


def over_all_2(share, axis, dim, apply):
    everything = lax.all_gather(share, axis, axis=dim, tiled=True)
    return apply(everything, jnp.int32(0))


def attention_part(attn_query, fresh_keys, fresh_values, stale_keys, stale_values, block_flags):
    length = attn_query.shape[0]
    heads_here = attn_query.shape[1] // HD
    row_flags = (jnp.repeat(block_flags, length // block_flags.shape[0]) == 1)[:, None]
    keys = jnp.where(row_flags, fresh_keys, stale_keys)
    values = jnp.where(row_flags, fresh_values, stale_values)
    queries = attn_query.reshape(length, heads_here, HD)
    scale = 1.0 / math.sqrt(HD)
    initial = (
        jnp.full((heads_here, length), -1e30, jnp.float32),
        jnp.zeros((heads_here, length), jnp.float32),
        jnp.zeros((heads_here, length, HD), jnp.float32),
    )
    carry = initial
    piece = (
        lax.all_gather(keys, "seq", axis=0, tiled=True),
        lax.all_gather(values, "seq", axis=0, tiled=True),
    )
    count = piece[0].shape[0]
    width = math.gcd(count, 512)
    key_blocks = piece[0].reshape(count // width, width, heads_here, HD)
    value_blocks = piece[1].reshape(count // width, width, heads_here, HD)

    def advance(state, blocks):
        highest, totals, weighted = state
        key_block, value_block = blocks
        scores = (
            jnp.einsum("qhd,khd->hqk", queries, key_block, preferred_element_type=jnp.float32)
            * scale
        )
        new_high = jnp.maximum(highest, jnp.max(scores, axis=-1))
        rescale = jnp.exp(highest - new_high)
        probs = jnp.exp(scores - new_high[:, :, None])
        totals = totals * rescale + jnp.sum(probs, axis=-1)
        weighted = weighted * rescale[:, :, None] + jnp.einsum(
            "hqk,khd->hqd",
            probs.astype(jnp.bfloat16),
            value_block,
            preferred_element_type=jnp.float32,
        )
        return ((new_high, totals, weighted), None)

    carry, unused = lax.scan(advance, carry, (key_blocks, value_blocks))
    highest, totals, weighted = carry
    mixed = weighted / totals[:, :, None]
    return jnp.transpose(mixed, (1, 0, 2)).reshape(length, heads_here * HD).astype(jnp.bfloat16)


def expert_part(moe_tokens, expert_ids, gate_weights, up_weight, up_bias, down_weight, down_bias):
    tokens_here, width = moe_tokens.shape
    choose = expert_ids.shape[1]
    number = lax.axis_size("seq") * up_weight.shape[0]
    capacity = 5 * tokens_here // (2 * number)
    flat_ids = expert_ids.reshape(-1)
    hits = (flat_ids[:, None] == jnp.arange(number, dtype=jnp.int32)[None, :]).astype(jnp.int32)
    before = jnp.cumsum(hits, axis=0) - hits
    place = jnp.sum(before * hits, axis=1)
    slot = flat_ids * capacity + place
    slot_pairs = slot.reshape(tokens_here, choose)
    table = jnp.sum(
        (
            slot_pairs[None, :, :] == jnp.arange(number * capacity, dtype=jnp.int32)[:, None, None]
        ).astype(jnp.int32),
        axis=-1,
    )
    buffer = jnp.dot(
        table.astype(jnp.bfloat16), moe_tokens, preferred_element_type=jnp.float32
    ).astype(jnp.bfloat16)
    buffer = buffer.reshape(number, capacity, width)
    received = lax.all_to_all(buffer, "seq", split_axis=0, concat_axis=0, tiled=True)
    sources = received.shape[0]
    count = received.shape[1]
    flat_rows = received.reshape(sources * count, width)
    chip_rows = lax.all_gather(flat_rows, "tp", axis=0, tiled=True)

    def project(piece):
        return jax.nn.gelu(
            jnp.dot(chip_rows, piece[0], preferred_element_type=jnp.float32) + piece[1]
        ).astype(jnp.bfloat16)

    hidden = over_all_2(
        (up_weight[0], up_bias[0][None, :].astype(jnp.bfloat16)),
        "exp",
        1,
        lambda piece, start: project((piece[0], piece[1].astype(jnp.float32))),
    )
    down_whole = lax.all_gather(down_weight[0], "exp", axis=0, tiled=True)
    summed = lax.psum_scatter(
        jnp.dot(hidden, down_whole, preferred_element_type=jnp.float32).astype(jnp.bfloat16),
        "tp",
        scatter_dimension=0,
        tiled=True,
    ).astype(jnp.float32)
    result = (summed + down_bias[0][None, :]).astype(jnp.bfloat16).reshape(sources, count, width)
    returned = lax.all_to_all(result, "seq", split_axis=0, concat_axis=0, tiled=True)
    flat_out = returned.reshape(number * capacity, width)
    picked = flat_out[slot].reshape(tokens_here, choose, width).astype(jnp.float32)
    combined = jnp.sum(picked * gate_weights[:, :, None], axis=1)
    return combined.astype(jnp.bfloat16)


def local(
    attn_query,
    fresh_keys,
    fresh_values,
    stale_keys,
    stale_values,
    block_flags,
    moe_tokens,
    expert_ids,
    gate_weights,
    up_weight,
    up_bias,
    down_weight,
    down_bias,
):
    attn_out = attention_part(
        attn_query, fresh_keys, fresh_values, stale_keys, stale_values, block_flags
    )
    moe_out = expert_part(
        moe_tokens, expert_ids, gate_weights, up_weight, up_bias, down_weight, down_bias
    )
    return (attn_out, moe_out)


def solution(mesh):
    in_specs = (
        P(("groups", "seq"), ("exp", "tp")),
        P(("groups", "seq"), ("exp", "tp")),
        P(("groups", "seq"), ("exp", "tp")),
        P(("groups", "seq"), ("exp", "tp")),
        P(("groups", "seq"), ("exp", "tp")),
        P(("groups", "seq")),
        P(("groups", "seq", "exp", "tp"), None),
        P(("groups", "seq", "exp", "tp"), None),
        P(("groups", "seq", "exp", "tp"), None),
        P("seq", None, ("exp", "tp")),
        P("seq", ("exp", "tp")),
        P("seq", ("exp", "tp"), None),
        P("seq", None),
    )
    out_specs = (P(("groups", "seq"), ("exp", "tp")), P(("groups", "seq", "exp", "tp"), None))
    return jax.shard_map(local, mesh=mesh, in_specs=in_specs, out_specs=out_specs, check_vma=False)
```

profile of v0, /device:TPU:0, one launch (start us, length us, event | category | flops | bytes accessed | tf_op | source)
XLA Modules:
  0.0 262.1 jit_solution(10440550585438227936)
XLA Ops:
  7.2 0.8 copy.32
  8.3 1.2 reduce-window.6
  10.6 25.3 %all_to_all.10 = bf16[4,80,1152]{2,1,0:T(8,128)(2,1)} all-to-all(bf16[4,80,1152]{2,1,0:T(8,128)(2,1)S(1)} %bitcast.82), channel_id=1, replica_groups=mesh['groups'=2,'seq'=4,'exp'=2,'tp'=2] {'seq'}, dimensions={0} | all-to-all | bytes 1474560 | tf_op jit(solution)/shard_map/all_to_all | solution.py:84
  36.0 0.7 all-gather.8.cloned.1.call-update
  37.5 4.4 %all_gather.22 = bf16[1,2304]{1,0:T(2,128)(2,1)S(1)} all-gather(bf16[1,1152]{1,0:T(2,128)(2,1)S(1)} %convert_element_type.61), channel_id=1, replica_groups=mesh['groups'=2,'seq'=4,'exp'=2,'tp'=2] {'exp'}, dimensions={1}, use_global_device_ids=true | all-gather | bytes 6912 | tf_op jit(solution)/shard_map/all_gather | solution.py:11
  41.9 3.0 %all-gather.6.cloned.1.call-done = bf16[640,1152]{1,0:T(8,128)(2,1)} async-done(((bf16[320,1152]{1,0:T(8,128)(2,1)}), bf16[640,1152]{1,0:T(8,128)(2,1)}) %all-gather.6.cloned.1.call-update) | async-done | bytes 1474576 | tf_op jit(solution)/shard_map/all_gather | solution.py:88
  44.9 72.0 %all-gather.8.cloned.1.call-done = bf16[1,1152,2304]{2,1,0:T(8,128)(2,1)} async-done(((bf16[1,1152,1152]{2,1,0:T(8,128)(2,1)}), bf16[1,1152,2304]{2,1,0:T(8,128)(2,1)}) %all-gather.8.cloned.1.call-update) | async-done | bytes 5308432 | tf_op jit(solution)/shard_map/all_gather | solution.py:11
  116.9 9.6 %fusion.22 = bf16[640,2304]{1,0:T(8,128)(2,1)} fusion(bf16[640,1152]{1,0:T(8,128)(2,1)} %all-gather.6.cloned.1.call-done, bf16[1,1152,2304]{2,1,0:T(8,128)(2,1)} %all-gather.8.cloned.1.call-done, f32[2304]{0:T(1024)S(1)} %convert_reduce_fusion.1), kind=kOutput, calls=%fused_computation.30 | convolution fusion | flops 3412131840 | bytes 9741312 | tf_op jit(solution)/shard_map/dot_general | solution.py:92
  126.5 61.3 %all-gather.10.cloned.1.call-done = bf16[1,2304,1152]{2,1,0:T(8,128)(2,1)} async-done(((bf16[1,1152,1152]{2,1,0:T(8,128)(2,1)}), bf16[1,2304,1152]{2,1,0:T(8,128)(2,1)}) %all-gather.10.cloned.1.call-update) | async-done | bytes 5308432 | tf_op jit(solution)/shard_map/all_gather | solution.py:101
  187.8 8.5 %fusion.29 = bf16[640,1152]{1,0:T(8,128)(2,1)} fusion(bf16[640,2304]{1,0:T(8,128)(2,1)} %fusion.22, bf16[1,2304,1152]{2,1,0:T(8,128)(2,1)} %all-gather.10.cloned.1.call-done), kind=kOutput, calls=%fused_computation.35 | convolution fusion | flops 3398123520 | bytes 9732096 | tf_op jit(solution)/shard_map/dot_general | solution.py:103
  196.5 16.5 %all_gather.18 = bf16[1024,288]{0,1:T(8,128)(2,1)S(1)} all-gather(bf16[256,288]{0,1:T(8,128)(2,1)S(1)} %get-tuple-element.101), channel_id=1, replica_groups=mesh['groups'=2,'seq'=4,'exp'=2,'tp'=2] {'seq'}, dimensions={0}, use_global_device_ids=true | all-gather | bytes 737280 | tf_op jit(solution)/shard_map/all_gather | solution.py:30
  213.5 0.9 copy.30
  214.4 16.1 %all_gather.19 = bf16[1024,288]{0,1:T(8,128)(2,1)S(1)} all-gather(bf16[256,288]{0,1:T(8,128)(2,1)S(1)} %get-tuple-element.100), channel_id=1, replica_groups=mesh['groups'=2,'seq'=4,'exp'=2,'tp'=2] {'seq'}, dimensions={0}, use_global_device_ids=true | all-gather | bytes 737280 | tf_op jit(solution)/shard_map/all_gather | solution.py:31
  230.9 0.9 copy.31
  231.9 2.1 add_convert_fusion
  234.0 4.9 %all-to-all-start.1 = ((bf16[4,80,1152]{2,1,0:T(8,128)(2,1)}), bf16[4,80,1152]{2,1,0:T(8,128)(2,1)S(1)}, u32[]{:S(2)}, u32[]{:S(2)}) async-start(bf16[4,80,1152]{2,1,0:T(8,128)(2,1)} %bitcast.10), calls=%async_computation.2 | async-start | bytes 1474560 | tf_op jit(solution)/shard_map/all_to_all | solution.py:109
  238.8 6.9 %while.15 = (s32[]{:T(128)}, f32[4,256]{1,0:T(4,128)S(1)}, f32[4,256]{1,0:T(4,128)S(1)}, f32[4,256,72]{1,2,0:T(8,128)S(1)}, bf16[2,512,4,72]{1,3,2,0:T(8,128)(2,...) while((s32[]{:T(128)}, f32[4,256]{1,0:T(4,128)S(1)}, ...), condition=%wide.region_3.4_spmd.clone, body=%wide.region_0.3_spmd.clone.sunk | while | flops 155415552 | bytes 7685225 | solution.py:57
  238.8 1.5 bitcast_reduce_fusion.2
  240.8 1.5 convolution_add_fusion.2
  242.3 1.5 bitcast_reduce_fusion.2
  244.2 1.5 convolution_add_fusion.2
  246.7 4.9 %all-to-all-done.1 = bf16[4,80,1152]{2,1,0:T(8,128)(2,1)S(1)} async-done(((bf16[4,80,1152]{2,1,0:T(8,128)(2,1)}), bf16[4,80,1152]{2,1,0:T(8,128)(2,1)S(1)}, u32[]{:S(2)}, u32[]{:S(2)}) %all-to-all-start.1) | async-done | bytes 737312 | tf_op jit(solution)/shard_map/all_to_all | solution.py:109
  251.6 1.3 gather_fusion
  253.4 2.2 multiply_reduce_fusion
  (66 shorter events, 5.6 us)
Async XLA Ops:
  7.2 3.1 %copy-start = (bf16[128,1152]{1,0:T(8,128)(2,1)S(1)}, bf16[128,1152]{1,0:T(8,128)(2,1)}, u32[]{:S(2)}) copy-start(bf16[128,1152]{1,0:T(8,128)(2,1)} %param.21) | copy-start | bytes 884740
  7.2 37.7 %all-gather.6.cloned.1.call-start = ((), (), s32[]{:S(2)}) async-start(), calls=%async_computation.3 | async-start | bytes 2211840 | tf_op jit(solution)/shard_map/all_gather | solution.py:88
  36.0 1.5 copy-start.5
  36.0 80.9 %all-gather.8.cloned.1.call-start = ((), (), s32[]{:S(2)}) async-start(), calls=%async_computation.5 | async-start | bytes 7962624 | tf_op jit(solution)/shard_map/all_gather | solution.py:11
  36.7 151.0 %all-gather.10.cloned.1.call-start = ((), (), s32[]{:S(2)}) async-start(), calls=%async_computation.6 | async-start | bytes 7962624 | tf_op jit(solution)/shard_map/all_gather | solution.py:101
  37.5 194.4 %reduce-scatter.2.cloned.1.call-start = ((), (), s32[]{:S(2)}) async-start(), calls=%async_computation.4 | async-start | bytes 2211840 | tf_op jit(solution)/shard_map/reduce_scatter | solution.py:102
  126.5 69.9 %copy-start.8 = (s32[2]{0:T(128)S(1)}, s32[2]{0:T(128)}, u32[]{:S(2)}) copy-start(s32[2]{0:T(128)} %param.20) | copy-start | bytes 28
  126.5 70.0 %copy-start.1 = (bf16[256,288]{0,1:T(8,128)(2,1)S(1)}, bf16[256,288]{0,1:T(8,128)(2,1)}, u32[]{:S(2)}) copy-start(bf16[256,288]{0,1:T(8,128)(2,1)} %param.17) | copy-start | bytes 442372
  126.5 70.0 %copy-start.2 = (bf16[256,288]{0,1:T(8,128)(2,1)S(1)}, bf16[256,288]{0,1:T(8,128)(2,1)}, u32[]{:S(2)}) copy-start(bf16[256,288]{0,1:T(8,128)(2,1)} %param.19) | copy-start | bytes 442372
  126.5 70.0 %copy-start.3 = (bf16[256,288]{0,1:T(8,128)(2,1)S(1)}, bf16[256,288]{0,1:T(8,128)(2,1)}, u32[]{:S(2)}) copy-start(bf16[256,288]{0,1:T(8,128)(2,1)} %param.16) | copy-start | bytes 442372
  126.5 70.0 %copy-start.4 = (bf16[256,288]{0,1:T(8,128)(2,1)S(1)}, bf16[256,288]{0,1:T(8,128)(2,1)}, u32[]{:S(2)}) copy-start(bf16[256,288]{0,1:T(8,128)(2,1)} %param.18) | copy-start | bytes 442372
  213.1 18.7 %copy-start.6 = (f32[1,1152]{1,0:T(1,128)S(1)}, f32[1,1152]{1,0:T(1,128)}, u32[]{:S(2)}) copy-start(f32[1,1152]{1,0:T(1,128)} %param.27) | copy-start | bytes 13828
  234.0 17.6 %all-to-all-start.1 = ((bf16[4,80,1152]{2,1,0:T(8,128)(2,1)}), bf16[4,80,1152]{2,1,0:T(8,128)(2,1)S(1)}, u32[]{:S(2)}, u32[]{:S(2)}) async-start(bf16[4,80,1152]{2,1,0:T(8,128)(2,1)} %bitcast.10), calls=%async_computation.2 | async-start | bytes 1474560 | tf_op jit(solution)/shard_map/all_to_all | solution.py:109
  238.8 7.0 %copy-start.7 = (f32[128,2]{0,1:T(2,128)S(1)}, f32[128,2]{0,1:T(2,128)}, u32[]{:S(2)}) copy-start(f32[128,2]{0,1:T(2,128)} %param.23) | copy-start | bytes 3076
Sparse Core Ops, SparseCore 0:
  36.1 8.7 all-gather.5
  46.4 70.4 all-gather.7
  118.5 69.2 all-gather.9
  196.5 8.9 reduce-scatter.1
where the time goes:
time: 263 us; the launch traced here: 262 us
  waiting for transfers between devices  143 us (54%)
  blocking collectives  62.3 us (24%)
  matrix products  24.4 us (9%)
  between operations  14 us (5%)
  other arithmetic  7.3 us (3%)
  local copies, waits for them, and re-layouts  6.41 us (2%)
  starting transfers between devices  5.02 us (2%)
    all_gather x1, waiting for transfers between devices, over_all_2(): everything = lax.all_gather(share, axis, axis=dim, tiled=True)  72 us
    all_gather x1, waiting for transfers between devices, expert_part(): down_whole = lax.all_gather(down_weight[0], 'exp', axis=0, tiled=True)  61.3 us
    all_to_all x1, blocking collectives, expert_part(): lax.all_to_all(buffer, 'seq', split_axis=0, concat_axis=0, tiled=True)  25.3 us
    all_gather x1, blocking collectives, attention_part(): lax.all_gather(keys, 'seq', axis=0, tiled=True)  16.5 us
    all_gather x1, blocking collectives, attention_part(): lax.all_gather(values, 'seq', axis=0, tiled=True)  16.1 us
    dot_general x1, matrix products, project(): jnp.dot(chip_rows, piece[0], preferred_element_type=jnp.float32) + piece[1]  9.57 us
    dot_general x1, matrix products, expert_part(): jnp.dot(hidden, down_whole, preferred_element_type=jnp.float32)  8.54 us
  transfers between devices with their start and end apart: 5, of which 4 were waited for; matrix products, arithmetic and copies ran while one was open for 8% of the time, Pallas kernels for 0%

commit v1 on v0

--- a/solution.py
+++ b/solution.py
@@ -5,6 +5,29 @@
 from jax.sharding import PartitionSpec as P
 
 HD = 72
+
+
+def joined_along(blocks, dim):
+    blocks = jnp.moveaxis(blocks, 0, dim)
+    shape = blocks.shape
+    return blocks.reshape(*shape[:dim], shape[dim] * shape[dim + 1], *shape[dim + 2 :])
+
+
+def doubled(x, axis):
+    peers, index = (lax.axis_size(axis), lax.axis_index(axis))
+    parts, bit = (x[None], 1)
+    while bit < peers:
+        partner_block = lax.ppermute(parts, axis, [(i, i ^ bit) for i in range(peers)])
+        low = index & bit == 0
+        parts = jnp.concatenate(
+            [jnp.where(low, parts, partner_block), jnp.where(low, partner_block, parts)]
+        )
+        bit *= 2
+    return parts
+
+
+def doubled_up(x, axis, dim):
+    return joined_along(doubled(x, axis), dim)
 
 
 def over_all_2(share, axis, dim, apply):
@@ -26,10 +49,7 @@
         jnp.zeros((heads_here, length, HD), jnp.float32),
     )
     carry = initial
-    piece = (
-        lax.all_gather(keys, "seq", axis=0, tiled=True),
-        lax.all_gather(values, "seq", axis=0, tiled=True),
-    )
+    piece = (lax.all_gather(keys, "seq", axis=0, tiled=True), doubled_up(values, "seq", 0))
     count = piece[0].shape[0]
     width = math.gcd(count, 512)
     key_blocks = piece[0].reshape(count // width, width, heads_here, HD)

time: 263 us -> 266 us (1.011)
  waiting for transfers between devices: 143 us -> 159 us
  blocking collectives: 62.3 us -> 47 us
    all_gather x1 -> x0, blocking collectives: 16.1 us -> none  [attention_part(): lax.all_gather(values, 'seq', axis=0, tiled=True)]
    ppermute x0 -> x2, waiting for transfers between devices: none -> 11.3 us  [doubled(): lax.ppermute(parts, axis, [(i, i ^ bit) for i in range(peers)])]
    all_to_all x1, waiting for transfers between devices: 4.88 us -> 10.3 us  [expert_part(): lax.all_to_all(result, 'seq', split_axis=0, concat_axis=0, tiled=True)]
  transfers between devices with their start and end apart: 5 -> 7, of which waited for: 4 -> 5; matrix products, arithmetic and copies ran while one was open for 8% -> 8% of each run, Pallas kernels for 0% -> 0%
where the time goes in v1:
time: 266 us; the launch traced here: 265 us
  waiting for transfers between devices  159 us (60%)
  blocking collectives  47 us (18%)
  matrix products  24.4 us (9%)
  between operations  14 us (5%)
  other arithmetic  7.48 us (3%)
  local copies, waits for them, and re-layouts  6.81 us (3%)
  starting transfers between devices  6.2 us (2%)
    all_gather x1, waiting for transfers between devices, over_all_2(): everything = lax.all_gather(share, axis, axis=dim, tiled=True)  72 us
    all_gather x1, waiting for transfers between devices, expert_part(): down_whole = lax.all_gather(down_weight[0], 'exp', axis=0, tiled=True)  61.2 us
    all_to_all x1, blocking collectives, expert_part(): lax.all_to_all(buffer, 'seq', split_axis=0, concat_axis=0, tiled=True)  25.3 us
    all_gather x1, blocking collectives, attention_part(): lax.all_gather(keys, 'seq', axis=0, tiled=True)  17.3 us
    ppermute x2, waiting for transfers between devices, doubled(): lax.ppermute(parts, axis, [(i, i ^ bit) for i in range(peers)])  11.3 us
    all_to_all x1, waiting for transfers between devices, expert_part(): lax.all_to_all(result, 'seq', split_axis=0, concat_axis=0, tiled=True)  10.3 us
    dot_general x1, matrix products, project(): jnp.dot(chip_rows, piece[0], preferred_element_type=jnp.float32) + piece[1]  9.58 us
    dot_general x1, matrix products, expert_part(): jnp.dot(hidden, down_whole, preferred_element_type=jnp.float32)  8.54 us
  transfers between devices with their start and end apart: 7, of which 5 were waited for; matrix products, arithmetic and copies ran while one was open for 8% of the time, Pallas kernels for 0%

profile of v1, /device:TPU:0, one launch (start us, length us, event | category | flops | bytes accessed | tf_op | source)
XLA Modules:
  0.0 265.3 jit_solution(3433209990215338623)
XLA Ops:
  8.3 1.2 reduce-window.6
  10.6 25.3 %all_to_all.10 = bf16[4,80,1152]{2,1,0:T(8,128)(2,1)} all-to-all(bf16[4,80,1152]{2,1,0:T(8,128)(2,1)S(1)} %bitcast.84), channel_id=1, replica_groups=mesh['groups'=2,'seq'=4,'exp'=2,'tp'=2] {'seq'}, dimensions={0} | all-to-all | bytes 1474560 | tf_op jit(solution)/shard_map/all_to_all | solution.py:104
  37.5 4.4 %all_gather.18 = bf16[1,2304]{1,0:T(2,128)(2,1)S(1)} all-gather(bf16[1,1152]{1,0:T(2,128)(2,1)S(1)} %convert_element_type.61), channel_id=1, replica_groups=mesh['groups'=2,'seq'=4,'exp'=2,'tp'=2] {'exp'}, dimensions={1}, use_global_device_ids=true | all-gather | bytes 6912 | tf_op jit(solution)/shard_map/all_gather | solution.py:34
  41.9 3.0 %all-gather.6.cloned.1.call-done = bf16[640,1152]{1,0:T(8,128)(2,1)} async-done(((bf16[320,1152]{1,0:T(8,128)(2,1)}), bf16[640,1152]{1,0:T(8,128)(2,1)}) %all-gather.6.cloned.1.call-update) | async-done | bytes 1474576 | tf_op jit(solution)/shard_map/all_gather | solution.py:108
  44.9 72.0 %all-gather.8.cloned.1.call-done = bf16[1,1152,2304]{2,1,0:T(8,128)(2,1)} async-done(((bf16[1,1152,1152]{2,1,0:T(8,128)(2,1)}), bf16[1,1152,2304]{2,1,0:T(8,128)(2,1)}) %all-gather.8.cloned.1.call-update) | async-done | bytes 5308432 | tf_op jit(solution)/shard_map/all_gather | solution.py:34
  116.9 9.6 %fusion.22 = bf16[640,2304]{1,0:T(8,128)(2,1)} fusion(bf16[640,1152]{1,0:T(8,128)(2,1)} %all-gather.6.cloned.1.call-done, bf16[1,1152,2304]{2,1,0:T(8,128)(2,1)} %all-gather.8.cloned.1.call-done, f32[2304]{0:T(1024)S(1)} %convert_reduce_fusion.1), kind=kOutput, calls=%fused_computation.30 | convolution fusion | flops 3412131840 | bytes 9741312 | tf_op jit(solution)/shard_map/dot_general | solution.py:112
  126.5 61.2 %all-gather.10.cloned.1.call-done = bf16[1,2304,1152]{2,1,0:T(8,128)(2,1)} async-done(((bf16[1,1152,1152]{2,1,0:T(8,128)(2,1)}), bf16[1,2304,1152]{2,1,0:T(8,128)(2,1)}) %all-gather.10.cloned.1.call-update) | async-done | bytes 5308432 | tf_op jit(solution)/shard_map/all_gather | solution.py:121
  187.8 8.5 %fusion.29 = bf16[640,1152]{1,0:T(8,128)(2,1)} fusion(bf16[640,2304]{1,0:T(8,128)(2,1)} %fusion.22, bf16[1,2304,1152]{2,1,0:T(8,128)(2,1)} %all-gather.10.cloned.1.call-done), kind=kOutput, calls=%fused_computation.35 | convolution fusion | flops 3398123520 | bytes 9732096 | tf_op jit(solution)/shard_map/dot_general | solution.py:123
  196.5 1.6 collective-permute-start
  198.1 17.3 %all_gather.15 = bf16[1024,288]{0,1:T(8,128)(2,1)S(1)} all-gather(bf16[256,288]{0,1:T(8,128)(2,1)S(1)} %get-tuple-element.105), channel_id=1, replica_groups=mesh['groups'=2,'seq'=4,'exp'=2,'tp'=2] {'seq'}, dimensions={0}, use_global_device_ids=true | all-gather | bytes 737280 | tf_op jit(solution)/shard_map/all_gather | solution.py:52
  215.8 0.9 copy.32
  217.1 0.8 collective-permute-start.1
  217.9 11.3 %collective-permute-done.1 = bf16[2,256,288]{1,2,0:T(8,128)(2,1)S(1)} collective-permute-done((bf16[2,256,288]{1,2,0:T(8,128)(2,1)S(1)}, bf16[2,256,288]{1,2,0:T(8,128)(2,1)S(1)}, u32[]{:S(2)}, u32[]{:S(2)}) %collective-permute-start.1) | collective-permute-done | bytes 294944 | tf_op jit(solution)/shard_map/ppermute | solution.py:20
  230.2 0.9 copy.33
  231.0 2.1 add_convert_fusion
  233.2 3.7 %all-to-all-start.1 = ((bf16[4,80,1152]{2,1,0:T(8,128)(2,1)}), bf16[4,80,1152]{2,1,0:T(8,128)(2,1)S(1)}, u32[]{:S(2)}, u32[]{:S(2)}) async-start(bf16[4,80,1152]{2,1,0:T(8,128)(2,1)} %bitcast.11), calls=%async_computation.2 | async-start | bytes 1474560 | tf_op jit(solution)/shard_map/all_to_all | solution.py:129
  236.8 6.9 %while.15 = (s32[]{:T(128)}, f32[4,256]{1,0:T(4,128)S(1)}, f32[4,256]{1,0:T(4,128)S(1)}, f32[4,256,72]{1,2,0:T(8,128)S(1)}, bf16[2,512,4,72]{1,3,2,0:T(8,128)(2,...) while((s32[]{:T(128)}, f32[4,256]{1,0:T(4,128)S(1)}, ...), condition=%wide.region_3.4_spmd.clone, body=%wide.region_0.3_spmd.clone.sunk | while | flops 155415552 | bytes 7685225 | solution.py:77
  236.8 1.5 bitcast_reduce_fusion.2
  238.8 1.5 convolution_add_fusion.2
  240.3 1.5 bitcast_reduce_fusion.2
  242.2 1.5 convolution_add_fusion.2
  244.4 10.3 %all-to-all-done.1 = bf16[4,80,1152]{2,1,0:T(8,128)(2,1)S(1)} async-done(((bf16[4,80,1152]{2,1,0:T(8,128)(2,1)}), bf16[4,80,1152]{2,1,0:T(8,128)(2,1)S(1)}, u32[]{:S(2)}, u32[]{:S(2)}) %all-to-all-start.1) | async-done | bytes 737312 | tf_op jit(solution)/shard_map/all_to_all | solution.py:129
  254.7 1.3 gather_fusion
  256.6 2.2 multiply_reduce_fusion
  (74 shorter events, 7.6 us)
Async XLA Ops:
  7.2 3.1 %copy-start = (bf16[128,1152]{1,0:T(8,128)(2,1)S(1)}, bf16[128,1152]{1,0:T(8,128)(2,1)}, u32[]{:S(2)}) copy-start(bf16[128,1152]{1,0:T(8,128)(2,1)} %param.21) | copy-start | bytes 884740
  7.2 37.7 %all-gather.6.cloned.1.call-start = ((), (), s32[]{:S(2)}) async-start(), calls=%async_computation.3 | async-start | bytes 2211840 | tf_op jit(solution)/shard_map/all_gather | solution.py:108
  36.0 1.5 copy-start.5
  36.0 80.9 %all-gather.8.cloned.1.call-start = ((), (), s32[]{:S(2)}) async-start(), calls=%async_computation.5 | async-start | bytes 7962624 | tf_op jit(solution)/shard_map/all_gather | solution.py:34
  36.7 151.0 %all-gather.10.cloned.1.call-start = ((), (), s32[]{:S(2)}) async-start(), calls=%async_computation.6 | async-start | bytes 7962624 | tf_op jit(solution)/shard_map/all_gather | solution.py:121
  37.5 193.6 %reduce-scatter.2.cloned.1.call-start = ((), (), s32[]{:S(2)}) async-start(), calls=%async_computation.4 | async-start | bytes 2211840 | tf_op jit(solution)/shard_map/reduce_scatter | solution.py:122
  126.5 69.8 %copy-start.8 = (s32[2]{0:T(128)S(1)}, s32[2]{0:T(128)}, u32[]{:S(2)}) copy-start(s32[2]{0:T(128)} %param.20) | copy-start | bytes 28
  126.5 69.9 %copy-start.1 = (bf16[256,288]{0,1:T(8,128)(2,1)S(1)}, bf16[256,288]{0,1:T(8,128)(2,1)}, u32[]{:S(2)}) copy-start(bf16[256,288]{0,1:T(8,128)(2,1)} %param.17) | copy-start | bytes 442372
  126.5 69.9 %copy-start.2 = (bf16[256,288]{0,1:T(8,128)(2,1)S(1)}, bf16[256,288]{0,1:T(8,128)(2,1)}, u32[]{:S(2)}) copy-start(bf16[256,288]{0,1:T(8,128)(2,1)} %param.19) | copy-start | bytes 442372
  126.5 69.9 %copy-start.3 = (bf16[256,288]{0,1:T(8,128)(2,1)S(1)}, bf16[256,288]{0,1:T(8,128)(2,1)}, u32[]{:S(2)}) copy-start(bf16[256,288]{0,1:T(8,128)(2,1)} %param.16) | copy-start | bytes 442372
  126.5 69.9 %copy-start.4 = (bf16[256,288]{0,1:T(8,128)(2,1)S(1)}, bf16[256,288]{0,1:T(8,128)(2,1)}, u32[]{:S(2)}) copy-start(bf16[256,288]{0,1:T(8,128)(2,1)} %param.18) | copy-start | bytes 442372
  196.3 20.5 %copy-start.7 = (f32[128,2]{0,1:T(2,128)S(1)}, f32[128,2]{0,1:T(2,128)}, u32[]{:S(2)}) copy-start(f32[128,2]{0,1:T(2,128)} %param.23) | copy-start | bytes 3076
  196.3 20.7 %copy-start.6 = (f32[1,1152]{1,0:T(1,128)S(1)}, f32[1,1152]{1,0:T(1,128)}, u32[]{:S(2)}) copy-start(f32[1,1152]{1,0:T(1,128)} %param.27) | copy-start | bytes 13828
  196.5 20.5 %collective-permute-start = (bf16[1,256,288]{1,2,0:T(8,128)(2,1)S(1)}, bf16[1,256,288]{1,2,0:T(8,128)(2,1)S(1)}, u32[]{:S(2)}, u32[]{:S(2)}) collective-permute-start(bf16[1,256,288]{1,2,0:T(8,128)(2,1)S(1)} %get-tuple-element.104), channel_id=1, source_target_pairs={{0,4},{4,0},{8,12},{12,8},{1,5},{5,1},{9,13},{13,9},{2,6},{6,2},{1... | collective-permute-start | bytes 442376 | tf_op jit(solution)/shard_map/ppermute | solution.py:20
  217.1 12.1 %collective-permute-start.1 = (bf16[2,256,288]{1,2,0:T(8,128)(2,1)S(1)}, bf16[2,256,288]{1,2,0:T(8,128)(2,1)S(1)}, u32[]{:S(2)}, u32[]{:S(2)}) collective-permute-start(bf16[2,256,288]{1,2,0:T(8,128)(2,1)S(1)} %pad_maximum_fusion.1), channel_id=1, source_target_pairs={{0,8},{4,12},{8,0},{12,4},{1,9},{5,13},{9,1},{13,5},{2,10},{6,14},... | collective-permute-start | bytes 884744 | tf_op jit(solution)/shard_map/ppermute | solution.py:20
  233.2 21.6 %all-to-all-start.1 = ((bf16[4,80,1152]{2,1,0:T(8,128)(2,1)}), bf16[4,80,1152]{2,1,0:T(8,128)(2,1)S(1)}, u32[]{:S(2)}, u32[]{:S(2)}) async-start(bf16[4,80,1152]{2,1,0:T(8,128)(2,1)} %bitcast.11), calls=%async_computation.2 | async-start | bytes 1474560 | tf_op jit(solution)/shard_map/all_to_all | solution.py:129
Sparse Core Ops, SparseCore 0:
  36.1 8.7 all-gather.5
  46.4 70.4 all-gather.7
  118.5 69.2 all-gather.9
  196.5 8.8 reduce-scatter.1
